TPU v7x, 32 devices: a whole 2x2x4 slice. The times are simulated.
32 devices in a mesh: rep: 4 (over y, x), feat: 8 (over z, core).
Axes of the slice: x: 2, y: 2, z: 4, core: 2. Of those that a mesh axis runs over, the one named last changes fastest.
Arguments:
- basis: float32 [4, 64, 32768], P('rep', None, 'feat'), may hold values from -6 to 6
- stream: bfloat16 [4, 2, 128, 32768], P('rep', None, None, 'feat'), may hold values from -6 to 6
Outputs:
- new_basis: float32 [4, 64, 32768], P('rep', None, 'feat')
All inputs are finite; a program needn't handle non-finite values.
Results may differ from a plain program's by a relative error of at most 0.0003.
Values sent between devices are 32-bit elements; how exact they have to be, the bound alone decides.
A program may use at most 64 MiB of HBM per device.

v0:
```python
import jax
import jax.numpy as jnp
from jax import lax
from jax.sharding import PartitionSpec as P

FEAT_DEV = 4096


learn_rate = 0.5


def high_dot(left, right):
    return jnp.dot(left, right, precision=lax.Precision.HIGHEST, preferred_element_type=jnp.float32)


def step_sum(partial_value):
    return lax.psum(partial_value, "feat")


def advance(current, proj, rows, step_size):
    cov = high_dot(proj.T, proj)
    drive = high_dot(proj.T, rows)
    shrink = high_dot(cov, current)
    return current + step_size * (drive - shrink)


def per_device(basis, stream):
    start = basis[0]
    batches = stream[0]
    steps_here = batches.shape[0]
    batch_rows = batches.shape[1]
    total_feat = FEAT_DEV * lax.axis_size("feat")
    scale = jnp.sqrt(jnp.float32(total_feat))
    step_size = learn_rate / batch_rows
    current = start
    for step in range(steps_here):
        rows = batches[step]
        proj = step_sum(high_dot(rows, current.T)) / scale
        current = advance(current, proj, rows, step_size)
    replicas = lax.axis_size("rep")
    average = lax.psum(basis, "rep")[0] / replicas
    mixed = current + average - start
    gram = lax.psum(high_dot(mixed, mixed.T), "feat") / total_feat
    lower = jnp.linalg.cholesky(gram)
    result = lax.linalg.triangular_solve(lower, mixed, left_side=True, lower=True)
    return result[None]


def solution(mesh):
    placed = (P("rep", None, "feat"), P("rep", None, None, "feat"))
    return jax.shard_map(
        per_device, mesh=mesh, in_specs=placed, out_specs=P("rep", None, "feat"), check_vma=False
    )
```

profile of v0, /device:TPU:0, one launch (start us, length us, event | category | flops | bytes accessed | tf_op | source)
XLA Modules:
  0.0 124.8 jit_solution(12542176621196448692)
XLA Ops:
  6.5 0.0 all-reduce.2.cloned.1.call-start
  6.5 0.7 all-reduce.2.cloned.1.call-update
  7.3 0.0 copy-start
  7.3 2.8 %fusion.11 = f32[128,64]{0,1:T(8,128)S(1)} fusion(f32[1,64,4096]{2,1,0:T(8,128)} %param.2, bf16[1,2,128,4096]{3,2,1,0:T(8,128)(2,1)} %param.3), kind=kOutput, calls=%fused_computation.15 | convolution fusion | flops 402653184 | bytes 2129920 | tf_op jit(solution)/shard_map/dot_general | solution.py:13
  10.1 30.3 %psum.28 = f32[128,64]{0,1:T(8,128)S(1)} all-reduce(f32[128,64]{0,1:T(8,128)S(1)} %fusion.11), channel_id=1, replica_groups=mesh['rep'=4,'feat'=8] {'feat'}, use_global_device_ids=true, to_apply=%region_0.0 | all-reduce | flops 8192 | bytes 65536 | tf_op jit(solution)/shard_map/psum | solution.py:17
  40.4 0.2 fusion.25
  40.6 1.8 %fusion.9 = f32[64,4096]{1,0:T(8,128)S(1)} fusion(bf16[1,2,128,4096]{3,2,1,0:T(8,128)(2,1)} %param.3, f32[128,64]{0,1:T(8,128)S(1)} %psum.28), kind=kOutput, calls=%fused_computation.13 | convolution fusion | flops 402661376 | bytes 2129920 | tf_op jit(solution)/shard_map/dot_general | solution.py:13
  42.4 0.0 copy-done
  42.4 0.0 copy-start.1
  42.4 1.1 fusion.3
  43.4 0.5 copy-done.1
  44.0 1.2 convolution_bitcast_fusion.1
  45.2 25.9 %psum.29 = f32[128,64]{0,1:T(8,128)S(1)} all-reduce(f32[128,64]{0,1:T(8,128)S(1)} %convolution_bitcast_fusion.1), channel_id=1, replica_groups=mesh['rep'=4,'feat'=8] {'feat'}, use_global_device_ids=true, to_apply=%region_1.0 | all-reduce | flops 8192 | bytes 65536 | tf_op jit(solution)/shard_map/psum | solution.py:17
  71.1 0.2 fusion.22
  71.3 2.8 %fusion.6 = f32[64,4096]{1,0:T(8,128)} fusion(bf16[1,2,128,4096]{3,2,1,0:T(8,128)(2,1)} %param.3, f32[128,64]{0,1:T(8,128)S(1)} %psum.29), kind=kOutput, calls=%fused_computation.10 | convolution fusion | flops 402661376 | bytes 2129920 | tf_op jit(solution)/shard_map/dot_general | solution.py:13
  74.1 0.0 all-reduce.2.cloned.1.call-done
  74.1 2.8 %fusion.5 = f32[64,4096]{1,0:T(8,128)S(1)} fusion(f32[64,4096]{1,0:T(8,128)S(1)} %fusion.3, f32[64,4096]{1,0:T(8,128)} %fusion.6, f32[64,64]{1,0:T(8,128)S(1)} %fusion.22, f32[1,64,4096]{2,1,0:T(8,128)S(1)} %copy-done, f32[1,64,4096]{2,1,0:T(8,128)} %all-reduce.2.cloned.1.call-done), kind=kOutput, calls=%fused_computation.7 | convolution fusion | flops 202899456 | bytes 5259264 | tf_op jit(solution)/shard_map/dot_general | solution.py:13
  76.8 1.0 fusion.36
  77.8 25.9 %psum.31 = f32[64,64]{0,1:T(8,128)S(1)} all-reduce(f32[64,64]{0,1:T(8,128)S(1)} %fusion.36), channel_id=1, replica_groups=mesh['rep'=4,'feat'=8] {'feat'}, use_global_device_ids=true, to_apply=%region_3.0 | all-reduce | flops 4096 | bytes 32768 | tf_op jit(solution)/shard_map/psum | solution.py:43
  103.8 0.1 copy.4
  103.9 5.8 %cholesky.16 = f32[64,64]{1,0:T(8,128)S(1)} custom-call(f32[64,64]{1,0:T(8,128)S(1)} %fusion.21), custom_call_target="Cholesky" | custom-call | tf_op jit(solution)/shard_map/jit(cholesky)/cholesky | solution.py:44
  109.7 0.6 compare_reduce_fusion
  110.4 0.7 fusion.19
  111.0 4.9 %custom-call.6 = f32[1,64,64]{1,2,0:T(8,128)S(1)} custom-call(f32[1,64,64]{2,1,0:T(8,128)S(1)} %fusion.19), custom_call_target="InvertDiagBlocksLowerTriangular" | custom-call | tf_op jit(solution)/shard_map/triangular_solve | solution.py:45
  115.9 2.0 %convolution_bitcast_fusion = f32[1,64,4096]{2,1,0:T(8,128)} fusion(f32[64,4096]{1,0:T(8,128)S(1)} %fusion.5, f32[1,64,64]{1,2,0:T(8,128)S(1)} %custom-call.6), kind=kOutput, calls=%fused_computation.8 | convolution fusion | flops 201326592 | bytes 2113536 | tf_op jit(solution)/shard_map/triangular_solve | solution.py:45
  (3 shorter events, 0.0 us)
Async XLA Ops:
  6.5 67.5 %all-reduce.2.cloned.1.call-start = ((), (), s32[]{:S(2)}) async-start(), calls=%async_computation | async-start | bytes 2097152 | tf_op jit(solution)/shard_map/psum | solution.py:41
  7.3 35.1 %copy-start = (f32[1,64,4096]{2,1,0:T(8,128)S(1)}, f32[1,64,4096]{2,1,0:T(8,128)}, u32[]{:S(2)}) copy-start(f32[1,64,4096]{2,1,0:T(8,128)} %param.2) | copy-start | bytes 3145732
  42.4 1.6 %copy-start.1 = (bf16[1,2,128,4096]{3,2,1,0:T(8,128)(2,1)S(1)}, bf16[1,2,128,4096]{3,2,1,0:T(8,128)(2,1)}, u32[]{:S(2)}) copy-start(bf16[1,2,128,4096]{3,2,1,0:T(8,128)(2,1)} %param.3) | copy-start | bytes 6291460
Sparse Core Ops, SparseCore 0:
  10.4 55.1 all-reduce.1
where the time goes:
time: 125 us
  blocking collectives  82.2 us (66%)
  matrix products  15.7 us (13%)
  between operations  13.5 us (11%)
  other arithmetic  12.1 us (10%)
    psum x2, blocking collectives, step_sum(): return lax.psum(partial_value, 'feat')  56.2 us
    psum x1, blocking collectives, per_device(): gram = lax.psum(high_dot(mixed, mixed.T), 'feat') / total_feat  25.9 us
    dot_general x9, matrix products, high_dot(): jnp.dot(left, right, precision=lax.Precision.HIGHEST, preferred_element_t...  13.7 us
    another operation x3, other arithmetic, per_device(): lower = jnp.linalg.cholesky(gram)  6.52 us
    another operation x2, other arithmetic, per_device(): lax.linalg.triangular_solve(lower, mixed, left_side=True, lower=True)  5.55 us
  transfers between devices with their start and end apart: 1, of which 0 were waited for; matrix products, arithmetic and copies ran while one was open for 8% of the time, Pallas kernels for 0%

commit v1 on v0

v1 whole, which is shorter than its diff:
```python
import functools

import jax
import jax.numpy as jnp
from jax import lax
from jax.experimental import pallas as pl
from jax.experimental.pallas import tpu as pltpu
from jax.sharding import PartitionSpec as P

learn_rate = 0.5
LANE = 128
MESH = pl.DeviceIdType.MESH
NN = (((1,), (0,)), ((), ()))
NT = (((1,), (1,)), ((), ()))


def exact_dot(left, right, dims):
    return lax.dot_general(
        left, right, dims, precision=lax.Precision.HIGHEST, preferred_element_type=jnp.float32
    )


def fast_dot(left, right, dims):
    return lax.dot_general(left, right, dims, preferred_element_type=jnp.float32)


def halves(value):
    high = value.astype(jnp.bfloat16)
    low = (value - high.astype(jnp.float32)).astype(jnp.bfloat16)
    return high, low


def gather_kernel(
    reps, feats, rank, rows, cols, total_feat,
    basis_hbm, stream_hbm, gram_ref, mixed_hbm,
    w_ref, x_ref, whl_ref, sums_refs, recv_refs, av_ref, m_ref,
    pay_ref, half_recv, half_sum, z_recv, full_ref,
    g_ref, g_core, g_sum, g_recv,
    load_sem, out_sem, ring_send, ring_recv, core_send, core_recv, z_send, z_recv_sem,
    gz_send, gz_recv,
):
    bits = reps.bit_length() - 1
    chunk = LANE * reps
    chunks = cols // chunk
    zs = feats // 2
    me = lax.axis_index("rep")
    feat = lax.axis_index("feat")
    core = feat % 2
    zpos = feat // 2
    eta = learn_rate / rows
    scale = jnp.sqrt(jnp.float32(total_feat))

    load_w = pltpu.make_async_copy(basis_hbm, w_ref, load_sem.at[0])
    load_w.start()
    load_x = pltpu.make_async_copy(stream_hbm, x_ref, load_sem.at[1])
    load_x.start()

    def rep_peer(b):
        bit = (me // (1 << b)) % 2
        return me + (1 - 2 * bit) * (1 << b), bit

    rep_ids = [(rep_peer(b)[0], feat) for b in range(bits)]
    core_id = (me, feat + 1 - 2 * core)
    z_ids = [(me, ((zpos + d) % zs) * 2 + core) for d in range(1, zs)]

    barrier = pltpu.get_barrier_semaphore()
    for peer in rep_ids + [core_id] + z_ids:
        pl.semaphore_signal(barrier, inc=1, device_id=peer, device_id_type=MESH)
    pl.semaphore_wait(barrier, bits + 1 + zs - 1)
    load_w.wait()

    def remote(src, dst, send_sem, recv_sem, peer):
        copy = pltpu.make_async_remote_copy(
            src_ref=src, dst_ref=dst, send_sem=send_sem, recv_sem=recv_sem,
            device_id=peer, device_id_type=MESH,
        )
        copy.start()
        return copy

    started = []

    def at(off, width):
        return pl.ds(pl.multiple_of(off, LANE), width)

    def order(c):
        return [(c + i) % bits for i in range(bits)]

    keeps = []
    for c in range(chunks):
        off = c * chunk
        rec = []
        for i, b in enumerate(order(c)):
            width = chunk >> (i + 1)
            bit = rep_peer(b)[1]
            off = off + bit * width
            rec.append(off)
        keeps.append(rec)

    ring = {}

    def send_scatter(c, i):
        b = order(c)[i]
        width = chunk >> (i + 1)
        bit = rep_peer(b)[1]
        other = (1 - bit) * width
        if i == 0:
            src = w_ref.at[:, at(c * chunk + other, width)]
        else:
            src = sums_refs[i - 1].at[:, at(c * 2 * width + other, width)]
        dst = recv_refs[i].at[:, c * width:(c + 1) * width]
        ring[c, i] = remote(src, dst, ring_send.at[i, c], ring_recv.at[i, c], rep_ids[b])

    def take_scatter(c, i):
        b = order(c)[i]
        width = chunk >> (i + 1)
        bit = rep_peer(b)[1]
        ring[c, i].wait_recv()
        if i == 0:
            own = w_ref[:, at(c * chunk + bit * width, width)]
        else:
            own = sums_refs[i - 1][:, at(c * 2 * width + bit * width, width)]
        total = own + recv_refs[i][:, c * width:(c + 1) * width]
        if i == bits - 1:
            av_ref[:, at(keeps[c][i], width)] = total / reps
        else:
            sums_refs[i][:, c * width:(c + 1) * width] = total

    def send_gather(c, i):
        s = bits - 1 - i
        b = order(c)[s]
        width = chunk >> (s + 1)
        piece = av_ref.at[:, at(keeps[c][s], width)]
        k = bits + i
        ring[c, k] = remote(piece, piece, ring_send.at[k, c], ring_recv.at[k, c], rep_ids[b])

    for c in range(chunks):
        send_scatter(c, 0)

    def step(c, i):
        if i < bits:
            take_scatter(c, i)
        else:
            ring[c, i].wait_recv()
        if i + 1 < bits:
            send_scatter(c, i + 1)
        elif i + 1 < 2 * bits:
            send_gather(c, i + 1 - bits)

    pending = [(c, i) for i in range(2 * bits - 1) for c in range(chunks)]
    place = [0]

    def advance(count):
        for _ in range(count):
            if place[0] < len(pending):
                step(*pending[place[0]])
                place[0] += 1

    high, low = halves(w_ref[...])
    whl_ref[0:rank, :] = high
    whl_ref[rank:2 * rank, :] = low
    load_x.wait()
    x_all = x_ref[...]
    wx = fast_dot(whl_ref[...], x_all, NT)
    wx = wx[0:rank] + wx[rank:2 * rank]
    pay_ref[0:rank, :] = wx[:, 0:rows]
    pay_ref[rank:2 * rank, :] = wx[:, rows:2 * rows]
    pay_ref[2 * rank:2 * rank + rows, :] = fast_dot(x_ref[0:rows, :], x_ref[rows:2 * rows, :], NT)

    half = rank + rows // 2
    give = pl.ds(pl.multiple_of((1 - core) * half, 8), half)
    keep = pl.ds(pl.multiple_of(core * half, 8), half)
    core_copy = remote(pay_ref.at[give, :], half_recv, core_send.at[0], core_recv.at[0], core_id)
    advance(chunks // 4)
    core_copy.wait_recv()
    half_sum[...] = pay_ref[keep, :] + half_recv[...]
    z_copies = [
        remote(half_sum, z_recv.at[d], z_send.at[d], z_recv_sem.at[d], z_ids[d])
        for d in range(zs - 1)
    ]
    started.append(core_copy)
    started.extend(z_copies)
    advance(chunks - chunks // 4 + chunks // 2)
    total = half_sum[...]
    for d in range(zs - 1):
        z_copies[d].wait_recv()
        total = total + z_recv[d]
    full_ref[keep, :] = total
    share = remote(full_ref.at[keep, :], full_ref.at[keep, :], core_send.at[1], core_recv.at[1], core_id)
    started.append(share)
    advance(chunks // 2)
    share.wait_recv()

    first = full_ref[0:rank, :]
    second = full_ref[rank:2 * rank, :]
    cross = full_ref[2 * rank:2 * rank + rows, :]
    proj0 = first / scale
    cov0 = exact_dot(proj0, proj0, NT)
    drive1 = exact_dot(proj0, cross, NN)
    proj1 = (second + eta * (drive1 - exact_dot(cov0, second, NN))) / scale
    cov1 = exact_dot(proj1, proj1, NT)
    advance(chunks // 2)
    k_w = eta * (eta * exact_dot(cov1, cov0, NN) - cov0 - cov1)
    k_x0 = eta * (proj0 - eta * exact_dot(cov1, proj0, NN))
    k_x1 = eta * proj1
    kwh, kwl = halves(k_w)
    kx = jnp.concatenate([k_x0, k_x1], axis=1)
    kxh, kxl = halves(kx)
    kx2 = jnp.concatenate([kxh, kxl], axis=0)
    kw2 = jnp.concatenate([kwh, kwl], axis=0)

    def unmixed(c):
        cut = slice(c * chunk, (c + 1) * chunk)
        part = fast_dot(kx2, x_ref[:, cut], NN) + fast_dot(kw2, whl_ref[0:rank, cut], NN)
        part = part[0:rank] + part[rank:2 * rank] + fast_dot(kwh, whl_ref[rank:2 * rank, cut], NN)
        m_ref[:, cut] = part

    for c in range(chunks):
        unmixed(c)
        advance(1)
    advance(len(pending))

    acc = jnp.zeros((2 * rank, rank), jnp.float32)
    outs = []
    for c in range(chunks):
        cut = slice(c * chunk, (c + 1) * chunk)
        ring[c, 2 * bits - 1].wait_recv()
        value = m_ref[:, cut] + av_ref[:, cut]
        m_ref[:, cut] = value
        copy = pltpu.make_async_copy(m_ref.at[:, cut], mixed_hbm.at[:, cut], out_sem.at[c])
        copy.start()
        outs.append(copy)
        mh, ml = halves(value)
        acc = acc + fast_dot(jnp.concatenate([mh, ml], axis=0), mh, NT)
    low_part = acc[rank:2 * rank]
    gram = (acc[0:rank] + (low_part + low_part.T)) / total_feat
    hr = rank // 2
    g_ref[...] = jnp.concatenate([gram[0:hr], gram[hr:rank]], axis=1)
    gc = remote(g_ref, g_core, core_send.at[2], core_recv.at[2], core_id)
    gc.wait_recv()
    g_sum[...] = g_ref[...] + g_core[...]
    g_copies = [
        remote(g_sum, g_recv.at[d], gz_send.at[d], gz_recv.at[d], z_ids[d]) for d in range(zs - 1)
    ]
    total = g_sum[...]
    for d in range(zs - 1):
        g_copies[d].wait_recv()
        total = total + g_recv[d]
    gram_ref[...] = total
    for copy in started + [gc] + g_copies + list(ring.values()):
        copy.wait_send()
    for copy in outs:
        copy.wait()


def solve_kernel(rank, cols, gram_ref, mixed_hbm, out_hbm, m_ref, o_ref, in_sem, out_sem):
    load = pltpu.make_async_copy(mixed_hbm, m_ref, in_sem.at[0])
    load.start()
    hr = rank // 2
    both = gram_ref[...]
    gram = jnp.concatenate([both[:, 0:rank], both[:, rank:2 * rank]], axis=0)
    eye = jnp.where(
        lax.broadcasted_iota(jnp.int32, (rank, rank), 0)
        == lax.broadcasted_iota(jnp.int32, (rank, rank), 1), 1.0, 0.0
    ).astype(jnp.float32)
    table = jnp.concatenate([gram, eye], axis=1)
    sub = 8
    blocks = [table[i * sub:(i + 1) * sub, :] for i in range(rank // sub)]
    ids = lax.broadcasted_iota(jnp.int32, (sub, 2 * rank), 0)
    for j in range(rank):
        b, r = divmod(j, sub)
        row = blocks[b][r:r + 1, :]
        inv = 1.0 / row[:, j:j + 1]
        scaled = row * inv
        for i in range(b, rank // sub):
            col = blocks[i][:, j:j + 1]
            update = col * scaled
            if i == b:
                update = jnp.where(ids > r, update, 0.0)
            blocks[i] = blocks[i] - update
    table = jnp.concatenate(blocks, axis=0)
    diag = jnp.sum(table[:, 0:rank] * eye, axis=1, keepdims=True)
    inverse = table[:, rank:2 * rank] * lax.rsqrt(diag)
    th, tl = halves(inverse)
    left = jnp.concatenate([th, th, tl], axis=1)
    load.wait()
    pieces = 4
    width = cols // pieces
    outs = []
    for p in range(pieces):
        cut = slice(p * width, (p + 1) * width)
        mh, ml = halves(m_ref[:, cut])
        o_ref[:, cut] = fast_dot(left, jnp.concatenate([mh, ml, mh], axis=0), NN)
        copy = pltpu.make_async_copy(o_ref.at[:, cut], out_hbm.at[:, cut], out_sem.at[p])
        copy.start()
        outs.append(copy)
    for copy in outs:
        copy.wait()


def per_device(basis, stream):
    reps = lax.axis_size("rep")
    feats = lax.axis_size("feat")
    start = basis[0]
    steps, rows, cols = stream.shape[1:]
    batches = stream[0].reshape(steps * rows, cols)
    rank = start.shape[0]
    bits = reps.bit_length() - 1
    chunk = LANE * reps
    chunks = cols // chunk
    zs = feats // 2
    half = rank + rows // 2
    f32 = jnp.float32
    vm = pltpu.VMEM
    hr = rank // 2
    dma = pltpu.SemaphoreType.DMA
    gram, mixed = pl.pallas_call(
        functools.partial(gather_kernel, reps, feats, rank, rows, cols, cols * feats),
        out_shape=(
            jax.ShapeDtypeStruct((hr, 2 * rank), f32),
            jax.ShapeDtypeStruct((rank, cols), f32),
        ),
        in_specs=[pl.BlockSpec(memory_space=pl.ANY)] * 2,
        out_specs=(pl.BlockSpec(memory_space=pltpu.VMEM), pl.BlockSpec(memory_space=pl.ANY)),
        scratch_shapes=[
            vm((rank, cols), f32),
            vm((steps * rows, cols), jnp.bfloat16),
            vm((2 * rank, cols), jnp.bfloat16),
            [vm((rank, cols >> (i + 1)), f32) for i in range(bits)],
            [vm((rank, cols >> (i + 1)), f32) for i in range(bits)],
            vm((rank, cols), f32),
            vm((rank, cols), f32),
            vm((2 * half, rows), f32),
            vm((half, rows), f32),
            vm((half, rows), f32),
            vm((zs - 1, half, rows), f32),
            vm((2 * half, rows), f32),
            vm((hr, 2 * rank), f32),
            vm((hr, 2 * rank), f32),
            vm((hr, 2 * rank), f32),
            vm((zs - 1, hr, 2 * rank), f32),
            dma((2,)),
            dma((chunks,)),
            dma((2 * bits, chunks)),
            dma((2 * bits, chunks)),
            dma((3,)),
            dma((3,)),
            dma((zs - 1,)),
            dma((zs - 1,)),
            dma((zs - 1,)),
            dma((zs - 1,)),
        ],
        compiler_params=pltpu.CompilerParams(collective_id=0, has_side_effects=True),
    )(start, batches)
    result = pl.pallas_call(
        functools.partial(solve_kernel, rank, cols),
        out_shape=jax.ShapeDtypeStruct((rank, cols), f32),
        in_specs=[pl.BlockSpec(memory_space=pltpu.VMEM), pl.BlockSpec(memory_space=pl.ANY)],
        out_specs=pl.BlockSpec(memory_space=pl.ANY),
        scratch_shapes=[vm((rank, cols), f32), vm((rank, cols), f32), dma((1,)), dma((4,))],
    )(gram, mixed)
    return result[None]


def solution(mesh):
    placed = (P("rep", None, "feat"), P("rep", None, None, "feat"))
    return jax.shard_map(
        per_device, mesh=mesh, in_specs=placed, out_specs=P("rep", None, "feat"), check_vma=False
    )
```

time: 125 us -> 39.6 us (0.32)
  blocking collectives: 82.2 us -> 0 us
  Pallas kernels: 0 us -> 39.4 us
  matrix products: 15.7 us -> 0 us
  between operations: 13.5 us -> 0.01 us
  other arithmetic: 12.1 us -> 0 us
    psum x3 -> x0, blocking collectives: 82.2 us -> none  [the longest x2 56.2 us: step_sum(): return lax.psum(partial_value, 'feat')]
    pallas_call x0 -> x2, Pallas kernels: none -> 39.4 us  [the longest x1 31.9 us: per_device(): pl.pallas_call(functools.partial(gather_kernel, reps, feats, rank, rows,...]
    dot_general x9 -> x0, matrix products: 13.7 us -> none  [high_dot(): jnp.dot(left, right, precision=lax.Precision.HIGHEST, preferred_element_t...]
    another operation x5 -> x0, other arithmetic: 12.1 us -> none  [the longest x3 6.52 us: per_device(): lower = jnp.linalg.cholesky(gram)]
    another operation x1 -> x0, matrix products: 2.02 us -> none  [per_device(): lax.linalg.triangular_solve(lower, mixed, left_side=True, lower=True)]
  transfers between devices with their start and end apart: 1 -> 0, of which waited for: 0 -> 0; matrix products, arithmetic and copies ran while one was open for 8% -> 0% of each run, Pallas kernels for 0% -> 0%
where the time goes in v1:
time: 39.6 us; the launch traced here: 39.4 us
  Pallas kernels  39.4 us (99%)
    pallas_call x1, Pallas kernels, per_device(): pl.pallas_call(functools.partial(gather_kernel, reps, feats, rank, rows,...  31.9 us
    pallas_call x1, Pallas kernels, per_device(): pl.pallas_call(functools.partial(solve_kernel, rank, cols), out_shape=jax...  7.48 us

profile of v1, /device:TPU:0, one launch (start us, length us, event | category | flops | bytes accessed | tf_op | source)
XLA Modules:
  0.0 39.4 jit_solution(8824558422877809036)
XLA Ops:
  0.0 31.9 %shard_map.28 = (f32[32,128]{1,0:T(8,128)}, f32[64,4096]{1,0:T(8,128)}) custom-call(f32[64,4096]{1,0:T(8,128)} %bitcast.4, bf16[256,4096]{1,0:T(8,128)(2,1)} %bitcast.3), custom_call_target="tpu_custom_call" | custom-call | tf_op jit(solution)/shard_map/pallas_call | solution.py:316
  31.9 7.5 %shard_map.29 = f32[64,4096]{1,0:T(8,128)} custom-call(f32[32,128]{1,0:T(8,128)} %get-tuple-element.7.gram_ref, f32[64,4096]{1,0:T(8,128)} %get-tuple-element.8.mixed_hbm), custom_call_target="tpu_custom_call" | custom-call | tf_op jit(solution)/shard_map/pallas_call | solution.py:354

commit v2 on v1

--- a/solution.py
+++ b/solution.py
@@ -9,6 +9,7 @@
 
 learn_rate = 0.5
 LANE = 128
+PLAN = (2, 18, 3, 1)
 MESH = pl.DeviceIdType.MESH
 NN = (((1,), (0,)), ((), ()))
 NT = (((1,), (1,)), ((), ()))
@@ -170,7 +171,7 @@
     give = pl.ds(pl.multiple_of((1 - core) * half, 8), half)
     keep = pl.ds(pl.multiple_of(core * half, 8), half)
     core_copy = remote(pay_ref.at[give, :], half_recv, core_send.at[0], core_recv.at[0], core_id)
-    advance(chunks // 4)
+    advance(PLAN[0])
     core_copy.wait_recv()
     half_sum[...] = pay_ref[keep, :] + half_recv[...]
     z_copies = [
@@ -179,7 +180,7 @@
     ]
     started.append(core_copy)
     started.extend(z_copies)
-    advance(chunks - chunks // 4 + chunks // 2)
+    advance(PLAN[1])
     total = half_sum[...]
     for d in range(zs - 1):
         z_copies[d].wait_recv()
@@ -187,7 +188,7 @@
     full_ref[keep, :] = total
     share = remote(full_ref.at[keep, :], full_ref.at[keep, :], core_send.at[1], core_recv.at[1], core_id)
     started.append(share)
-    advance(chunks // 2)
+    advance(PLAN[2])
     share.wait_recv()
 
     first = full_ref[0:rank, :]
@@ -198,7 +199,7 @@
     drive1 = exact_dot(proj0, cross, NN)
     proj1 = (second + eta * (drive1 - exact_dot(cov0, second, NN))) / scale
     cov1 = exact_dot(proj1, proj1, NT)
-    advance(chunks // 2)
+    advance(PLAN[3])
     k_w = eta * (eta * exact_dot(cov1, cov0, NN) - cov0 - cov1)
     k_x0 = eta * (proj0 - eta * exact_dot(cov1, proj0, NN))
     k_x1 = eta * proj1
@@ -266,17 +267,48 @@
     sub = 8
     blocks = [table[i * sub:(i + 1) * sub, :] for i in range(rank // sub)]
     ids = lax.broadcasted_iota(jnp.int32, (sub, 2 * rank), 0)
-    for j in range(rank):
+    for j in range(0, rank, 4):
         b, r = divmod(j, sub)
-        row = blocks[b][r:r + 1, :]
-        inv = 1.0 / row[:, j:j + 1]
-        scaled = row * inv
-        for i in range(b, rank // sub):
-            col = blocks[i][:, j:j + 1]
-            update = col * scaled
+        todo = range(b if r == 0 else b + 1, rank // sub)
+        lanes = [jnp.broadcast_to(blocks[b][:, j + k:j + k + 1], (sub, 2 * rank)) for k in range(4)]
+        cols4 = {
+            i: [jnp.broadcast_to(blocks[i][:, j + k:j + k + 1], (sub, 2 * rank)) for k in range(4)]
+            for i in todo if i != b
+        }
+        cols4[b] = lanes
+        rows4 = [blocks[b][r + k:r + k + 1, :] for k in range(4)]
+        d = [[lanes[l][r + k:r + k + 1, :] for l in range(4)] for k in range(4)]
+        idet = 1.0 / (d[0][0] * d[1][1] - d[0][1] * d[1][0])
+        i00, i01, i11 = d[1][1] * idet, -d[0][1] * idet, d[0][0] * idet
+        y0 = i00 * rows4[0] + i01 * rows4[1]
+        y1 = i01 * rows4[0] + i11 * rows4[1]
+        y02, y12 = i00 * d[0][2] + i01 * d[1][2], i01 * d[0][2] + i11 * d[1][2]
+        y03, y13 = i00 * d[0][3] + i01 * d[1][3], i01 * d[0][3] + i11 * d[1][3]
+        e22 = d[2][2] - (d[2][0] * y02 + d[2][1] * y12)
+        e23 = d[2][3] - (d[2][0] * y03 + d[2][1] * y13)
+        e33 = d[3][3] - (d[3][0] * y03 + d[3][1] * y13)
+        row2 = rows4[2] - (d[2][0] * y0 + d[2][1] * y1)
+        row3 = rows4[3] - (d[3][0] * y0 + d[3][1] * y1)
+        jdet = 1.0 / (e22 * e33 - e23 * e23)
+        j00, j01, j11 = e33 * jdet, -e23 * jdet, e22 * jdet
+        z0 = j00 * row2 + j01 * row3
+        z1 = j01 * row2 + j11 * row3
+        for i in todo:
+            c = cols4[i]
+            c2 = c[2] - (c[0] * y02 + c[1] * y12)
+            c3 = c[3] - (c[0] * y03 + c[1] * y13)
+            update = (c[0] * y0 + c[1] * y1) + (c2 * z0 + c3 * z1)
             if i == b:
-                update = jnp.where(ids > r, update, 0.0)
+                update = jnp.where(ids > r + 3, update, 0.0)
             blocks[i] = blocks[i] - update
+        done = [
+            rows4[0], rows4[1] - (d[0][1] / d[0][0]) * rows4[0],
+            row2, row3 - (e23 / e22) * row2,
+        ]
+        block = blocks[b]
+        for k in range(4):
+            block = jnp.where(ids == r + k, done[k], block)
+        blocks[b] = block
     table = jnp.concatenate(blocks, axis=0)
     diag = jnp.sum(table[:, 0:rank] * eye, axis=1, keepdims=True)
     inverse = table[:, rank:2 * rank] * lax.rsqrt(diag)

time: 39.6 us -> 34.1 us (0.86)
  Pallas kernels: 39.4 us -> 33.9 us
    pallas_call x1, Pallas kernels: 7.48 us -> 4.21 us  [per_device(): pl.pallas_call(functools.partial(solve_kernel, rank, cols), out_shape=jax...]
    pallas_call x1, Pallas kernels: 31.9 us -> 29.7 us  [per_device(): pl.pallas_call(functools.partial(gather_kernel, reps, feats, rank, rows,...]
where the time goes in v2:
time: 34.1 us; the launch traced here: 33.9 us
  Pallas kernels  33.9 us (99%)
    pallas_call x1, Pallas kernels, per_device(): pl.pallas_call(functools.partial(gather_kernel, reps, feats, rank, rows,...  29.7 us
    pallas_call x1, Pallas kernels, per_device(): pl.pallas_call(functools.partial(solve_kernel, rank, cols), out_shape=jax...  4.21 us

profile of v2, /device:TPU:0, one launch (start us, length us, event | category | flops | bytes accessed | tf_op | source)
XLA Modules:
  0.0 33.9 jit_solution(12384135172716521732)
XLA Ops:
  0.0 29.7 %shard_map.28 = (f32[32,128]{1,0:T(8,128)}, f32[64,4096]{1,0:T(8,128)}) custom-call(f32[64,4096]{1,0:T(8,128)} %bitcast.4, bf16[256,4096]{1,0:T(8,128)(2,1)} %bitcast.3), custom_call_target="tpu_custom_call" | custom-call | tf_op jit(solution)/shard_map/pallas_call | solution.py:348
  29.7 4.2 %shard_map.29 = f32[64,4096]{1,0:T(8,128)} custom-call(f32[32,128]{1,0:T(8,128)} %get-tuple-element.7.gram_ref, f32[64,4096]{1,0:T(8,128)} %get-tuple-element.8.mixed_hbm), custom_call_target="tpu_custom_call" | custom-call | tf_op jit(solution)/shard_map/pallas_call | solution.py:386

commit v3 on v2

--- a/solution.py
+++ b/solution.py
@@ -33,12 +33,12 @@
 
 def gather_kernel(
     reps, feats, rank, rows, cols, total_feat,
-    basis_hbm, stream_hbm, gram_ref, mixed_hbm,
-    w_ref, x_ref, whl_ref, sums_refs, recv_refs, av_ref, m_ref,
+    basis_hbm, stream_hbm, gram_ref, m_ref,
+    w_ref, x_ref, whl_ref, sums_refs, recv_refs, av_ref,
     pay_ref, half_recv, half_sum, z_recv, full_ref,
     g_ref, g_core, g_sum, g_recv,
-    load_sem, out_sem, ring_send, ring_recv, core_send, core_recv, z_send, z_recv_sem,
-    gz_send, gz_recv,
+    load_sem, ring_send, ring_recv, core_send, core_recv, z_send, z_recv_sem,
+    gz_send, gz_recv, hello_sem,
 ):
     bits = reps.bit_length() - 1
     chunk = LANE * reps
@@ -51,9 +51,12 @@
     eta = learn_rate / rows
     scale = jnp.sqrt(jnp.float32(total_feat))
 
-    load_w = pltpu.make_async_copy(basis_hbm, w_ref, load_sem.at[0])
-    load_w.start()
-    load_x = pltpu.make_async_copy(stream_hbm, x_ref, load_sem.at[1])
+    loads = []
+    for c in range(chunks):
+        cut = slice(c * chunk, (c + 1) * chunk)
+        loads.append(pltpu.make_async_copy(basis_hbm.at[:, cut], w_ref.at[:, cut], load_sem.at[c]))
+        loads[c].start()
+    load_x = pltpu.make_async_copy(stream_hbm, x_ref, load_sem.at[chunks])
     load_x.start()
 
     def rep_peer(b):
@@ -64,11 +67,22 @@
     core_id = (me, feat + 1 - 2 * core)
     z_ids = [(me, ((zpos + d) % zs) * 2 + core) for d in range(1, zs)]
 
+    beside = (zpos > 0).astype(jnp.int32) + (zpos < zs - 1).astype(jnp.int32)
+
+    def tell_beside(sem):
+        for ahead, there in ((-1, zpos > 0), (1, zpos < zs - 1)):
+
+            @pl.when(there)
+            def _():
+                pl.semaphore_signal(
+                    sem, inc=1, device_id=(me, feat + 2 * ahead), device_id_type=MESH
+                )
+
     barrier = pltpu.get_barrier_semaphore()
-    for peer in rep_ids + [core_id] + z_ids:
+    for peer in rep_ids + [core_id]:
         pl.semaphore_signal(barrier, inc=1, device_id=peer, device_id_type=MESH)
-    pl.semaphore_wait(barrier, bits + 1 + zs - 1)
-    load_w.wait()
+    tell_beside(barrier)
+    pl.semaphore_wait(barrier, bits + 1 + beside)
 
     def remote(src, dst, send_sem, recv_sem, peer):
         copy = pltpu.make_async_remote_copy(
@@ -135,7 +149,11 @@
         ring[c, k] = remote(piece, piece, ring_send.at[k, c], ring_recv.at[k, c], rep_ids[b])
 
     for c in range(chunks):
+        loads[c].wait()
         send_scatter(c, 0)
+    rounds = zs - 2
+    if rounds > 0:
+        tell_beside(hello_sem.at[0])
 
     def step(c, i):
         if i < bits:
@@ -174,6 +192,10 @@
     advance(PLAN[0])
     core_copy.wait_recv()
     half_sum[...] = pay_ref[keep, :] + half_recv[...]
+    for k in range(rounds):
+        pl.semaphore_wait(hello_sem.at[k], beside)
+        if k + 1 < rounds:
+            tell_beside(hello_sem.at[k + 1])
     z_copies = [
         remote(half_sum, z_recv.at[d], z_send.at[d], z_recv_sem.at[d], z_ids[d])
         for d in range(zs - 1)
@@ -221,15 +243,11 @@
     advance(len(pending))
 
     acc = jnp.zeros((2 * rank, rank), jnp.float32)
-    outs = []
     for c in range(chunks):
         cut = slice(c * chunk, (c + 1) * chunk)
         ring[c, 2 * bits - 1].wait_recv()
         value = m_ref[:, cut] + av_ref[:, cut]
         m_ref[:, cut] = value
-        copy = pltpu.make_async_copy(m_ref.at[:, cut], mixed_hbm.at[:, cut], out_sem.at[c])
-        copy.start()
-        outs.append(copy)
         mh, ml = halves(value)
         acc = acc + fast_dot(jnp.concatenate([mh, ml], axis=0), mh, NT)
     low_part = acc[rank:2 * rank]
@@ -249,13 +267,9 @@
     gram_ref[...] = total
     for copy in started + [gc] + g_copies + list(ring.values()):
         copy.wait_send()
-    for copy in outs:
-        copy.wait()
-
-
-def solve_kernel(rank, cols, gram_ref, mixed_hbm, out_hbm, m_ref, o_ref, in_sem, out_sem):
-    load = pltpu.make_async_copy(mixed_hbm, m_ref, in_sem.at[0])
-    load.start()
+
+
+def solve_kernel(rank, cols, gram_ref, m_ref, out_hbm, o_ref, out_sem):
     hr = rank // 2
     both = gram_ref[...]
     gram = jnp.concatenate([both[:, 0:rank], both[:, rank:2 * rank]], axis=0)
@@ -314,7 +328,6 @@
     inverse = table[:, rank:2 * rank] * lax.rsqrt(diag)
     th, tl = halves(inverse)
     left = jnp.concatenate([th, th, tl], axis=1)
-    load.wait()
     pieces = 4
     width = cols // pieces
     outs = []
@@ -348,18 +361,17 @@
     gram, mixed = pl.pallas_call(
         functools.partial(gather_kernel, reps, feats, rank, rows, cols, cols * feats),
         out_shape=(
-            jax.ShapeDtypeStruct((hr, 2 * rank), f32),
-            jax.ShapeDtypeStruct((rank, cols), f32),
+            pltpu.VMEM((hr, 2 * rank), f32),
+            pltpu.VMEM((rank, cols), f32),
         ),
         in_specs=[pl.BlockSpec(memory_space=pl.ANY)] * 2,
-        out_specs=(pl.BlockSpec(memory_space=pltpu.VMEM), pl.BlockSpec(memory_space=pl.ANY)),
+        out_specs=(pl.BlockSpec(memory_space=pltpu.VMEM), pl.BlockSpec(memory_space=pltpu.VMEM)),
         scratch_shapes=[
             vm((rank, cols), f32),
             vm((steps * rows, cols), jnp.bfloat16),
             vm((2 * rank, cols), jnp.bfloat16),
             [vm((rank, cols >> (i + 1)), f32) for i in range(bits)],
             [vm((rank, cols >> (i + 1)), f32) for i in range(bits)],
-            vm((rank, cols), f32),
             vm((rank, cols), f32),
             vm((2 * half, rows), f32),
             vm((half, rows), f32),
@@ -370,8 +382,7 @@
             vm((hr, 2 * rank), f32),
             vm((hr, 2 * rank), f32),
             vm((zs - 1, hr, 2 * rank), f32),
-            dma((2,)),
-            dma((chunks,)),
+            dma((chunks + 1,)),
             dma((2 * bits, chunks)),
             dma((2 * bits, chunks)),
             dma((3,)),
@@ -380,16 +391,20 @@
             dma((zs - 1,)),
             dma((zs - 1,)),
             dma((zs - 1,)),
+            pltpu.SemaphoreType.REGULAR((max(zs - 2, 1),)),
         ],
         compiler_params=pltpu.CompilerParams(collective_id=0, has_side_effects=True),
     )(start, batches)
     result = pl.pallas_call(
         functools.partial(solve_kernel, rank, cols),
         out_shape=jax.ShapeDtypeStruct((rank, cols), f32),
-        in_specs=[pl.BlockSpec(memory_space=pltpu.VMEM), pl.BlockSpec(memory_space=pl.ANY)],
+        in_specs=[pl.BlockSpec(memory_space=pltpu.VMEM)] * 2,
         out_specs=pl.BlockSpec(memory_space=pl.ANY),
-        scratch_shapes=[vm((rank, cols), f32), vm((rank, cols), f32), dma((1,)), dma((4,))],
-    )(gram, mixed)
+        scratch_shapes=[vm((rank, cols), f32), dma((4,))],
+    )(
+        pltpu.with_memory_space_constraint(gram, pltpu.VMEM),
+        pltpu.with_memory_space_constraint(mixed, pltpu.VMEM),
+    )
     return result[None]
 
 

time: 34.1 us -> 32.5 us (0.953)
  Pallas kernels: 33.9 us -> 32.3 us
    pallas_call x1, Pallas kernels: 4.21 us -> 3.41 us  [per_device(): pl.pallas_call(functools.partial(solve_kernel, rank, cols), out_shape=jax...]
    pallas_call x1, Pallas kernels: 29.7 us -> 28.9 us  [per_device(): pl.pallas_call(functools.partial(gather_kernel, reps, feats, rank, rows,...]
where the time goes in v3:
time: 32.5 us; the launch traced here: 32.3 us
  Pallas kernels  32.3 us (99%)
    pallas_call x1, Pallas kernels, per_device(): pl.pallas_call(functools.partial(gather_kernel, reps, feats, rank, rows,...  28.9 us
    pallas_call x1, Pallas kernels, per_device(): pl.pallas_call(functools.partial(solve_kernel, rank, cols), out_shape=jax...  3.41 us

profile of v3, /device:TPU:0, one launch (start us, length us, event | category | flops | bytes accessed | tf_op | source)
XLA Modules:
  0.0 32.3 jit_solution(9574913465776025343)
XLA Ops:
  0.0 28.9 %shard_map.28 = (f32[32,128]{1,0:T(8,128)S(1)}, f32[64,4096]{1,0:T(8,128)S(1)}) custom-call(f32[64,4096]{1,0:T(8,128)} %bitcast.4, bf16[256,4096]{1,0:T(8,128)(2,1)} %bitcast.3), custom_call_target="tpu_custom_call" | custom-call | tf_op jit(solution)/shard_map/pallas_call | solution.py:361
  28.9 3.4 %shard_map.29 = f32[64,4096]{1,0:T(8,128)} custom-call(f32[32,128]{1,0:T(8,128)S(1)} %get-tuple-element.7.gram_ref, f32[64,4096]{1,0:T(8,128)S(1)} %get-tuple-element.8.m_ref), custom_call_target="tpu_custom_call" | custom-call | tf_op jit(solution)/shard_map/pallas_call | solution.py:398

commit v4 on v3

--- a/solution.py
+++ b/solution.py
@@ -242,14 +242,22 @@
         advance(1)
     advance(len(pending))
 
-    acc = jnp.zeros((2 * rank, rank), jnp.float32)
-    for c in range(chunks):
-        cut = slice(c * chunk, (c + 1) * chunk)
-        ring[c, 2 * bits - 1].wait_recv()
+    acc = [jnp.zeros((2 * rank, rank), jnp.float32)]
+
+    def mix(off, width):
+        cut = at(off, width)
         value = m_ref[:, cut] + av_ref[:, cut]
         m_ref[:, cut] = value
         mh, ml = halves(value)
-        acc = acc + fast_dot(jnp.concatenate([mh, ml], axis=0), mh, NT)
+        acc[0] = acc[0] + fast_dot(jnp.concatenate([mh, ml], axis=0), mh, NT)
+
+    wide = chunk // 2
+    for c in range(chunks):
+        mix(keeps[c][0], wide)
+    for c in range(chunks):
+        ring[c, 2 * bits - 1].wait_recv()
+        mix(2 * c * chunk + wide - keeps[c][0], wide)
+    acc = acc[0]
     low_part = acc[rank:2 * rank]
     gram = (acc[0:rank] + (low_part + low_part.T)) / total_feat
     hr = rank // 2
@@ -281,7 +289,28 @@
     sub = 8
     blocks = [table[i * sub:(i + 1) * sub, :] for i in range(rank // sub)]
     ids = lax.broadcasted_iota(jnp.int32, (sub, 2 * rank), 0)
+    pieces = 4
+    width = cols // pieces
+    outs = []
+
+    def finish(lo, hi):
+        part = jnp.concatenate(blocks[lo // sub:hi // sub], axis=0)
+        diag = jnp.sum(part[:, 0:rank] * eye[lo:hi], axis=1, keepdims=True)
+        th, tl = halves(part[:, rank:rank + hi] * lax.rsqrt(diag))
+        left = jnp.concatenate([th, th, tl], axis=1)
+        for p in range(pieces):
+            cut = slice(p * width, (p + 1) * width)
+            mh, ml = halves(m_ref[0:hi, cut])
+            o_ref[lo:hi, cut] = fast_dot(left, jnp.concatenate([mh, ml, mh], axis=0), NN)
+            copy = pltpu.make_async_copy(
+                o_ref.at[lo:hi, cut], out_hbm.at[lo:hi, cut], out_sem.at[len(outs)]
+            )
+            copy.start()
+            outs.append(copy)
+
     for j in range(0, rank, 4):
+        if j == hr:
+            finish(0, hr)
         b, r = divmod(j, sub)
         todo = range(b if r == 0 else b + 1, rank // sub)
         lanes = [jnp.broadcast_to(blocks[b][:, j + k:j + k + 1], (sub, 2 * rank)) for k in range(4)]
@@ -323,21 +352,7 @@
         for k in range(4):
             block = jnp.where(ids == r + k, done[k], block)
         blocks[b] = block
-    table = jnp.concatenate(blocks, axis=0)
-    diag = jnp.sum(table[:, 0:rank] * eye, axis=1, keepdims=True)
-    inverse = table[:, rank:2 * rank] * lax.rsqrt(diag)
-    th, tl = halves(inverse)
-    left = jnp.concatenate([th, th, tl], axis=1)
-    pieces = 4
-    width = cols // pieces
-    outs = []
-    for p in range(pieces):
-        cut = slice(p * width, (p + 1) * width)
-        mh, ml = halves(m_ref[:, cut])
-        o_ref[:, cut] = fast_dot(left, jnp.concatenate([mh, ml, mh], axis=0), NN)
-        copy = pltpu.make_async_copy(o_ref.at[:, cut], out_hbm.at[:, cut], out_sem.at[p])
-        copy.start()
-        outs.append(copy)
+    finish(hr, rank)
     for copy in outs:
         copy.wait()
 
@@ -400,7 +415,7 @@
         out_shape=jax.ShapeDtypeStruct((rank, cols), f32),
         in_specs=[pl.BlockSpec(memory_space=pltpu.VMEM)] * 2,
         out_specs=pl.BlockSpec(memory_space=pl.ANY),
-        scratch_shapes=[vm((rank, cols), f32), dma((4,))],
+        scratch_shapes=[vm((rank, cols), f32), dma((8,))],
     )(
         pltpu.with_memory_space_constraint(gram, pltpu.VMEM),
         pltpu.with_memory_space_constraint(mixed, pltpu.VMEM),

time: 32.5 us -> 32.4 us (level)
  no operation moved by 1% of the time
where the time goes in v4:
time: 32.4 us; the launch traced here: 32.2 us
  Pallas kernels  32.2 us (99%)
    pallas_call x1, Pallas kernels, per_device(): pl.pallas_call(functools.partial(gather_kernel, reps, feats, rank, rows,...  28.8 us
    pallas_call x1, Pallas kernels, per_device(): pl.pallas_call(functools.partial(solve_kernel, rank, cols), out_shape=jax...  3.38 us

profile of v4, /device:TPU:0, one launch (start us, length us, event | category | flops | bytes accessed | tf_op | source)
XLA Modules:
  0.0 32.2 jit_solution(2264390354014692614)
XLA Ops:
  0.0 28.8 %shard_map.28 = (f32[32,128]{1,0:T(8,128)S(1)}, f32[64,4096]{1,0:T(8,128)S(1)}) custom-call(f32[64,4096]{1,0:T(8,128)} %bitcast.4, bf16[256,4096]{1,0:T(8,128)(2,1)} %bitcast.3), custom_call_target="tpu_custom_call" | custom-call | tf_op jit(solution)/shard_map/pallas_call | solution.py:376
  28.9 3.4 %shard_map.29 = f32[64,4096]{1,0:T(8,128)} custom-call(f32[32,128]{1,0:T(8,128)S(1)} %get-tuple-element.7.gram_ref, f32[64,4096]{1,0:T(8,128)S(1)} %get-tuple-element.8.m_ref), custom_call_target="tpu_custom_call" | custom-call | tf_op jit(solution)/shard_map/pallas_call | solution.py:413
